TPU v7x, 256 devices: a whole 4x4x8 slice. The times are simulated.
256 devices in a mesh: expert: 8 (over y_lo, x), rep: 32 (over z, y_hi, core).
Axes of the slice: x: 4, y: 4 (y_hi: 2, y_lo: 2; y = y_hi * 2 + y_lo), z: 8, core: 2. Of those that a mesh axis runs over, the one named last changes fastest.
Arguments:
- route_ids: int32 [2048, 2], P(('expert', 'rep')), may hold values from 0 to 7, all different within a row; in each aligned block of 8 rows (0 to 7, 8 to 15, ...) at most 4 rows name the same one
- route_weight: float32 [2048, 2], P(('expert', 'rep')), may hold values from 0.2 to 0.8
- input_float: bfloat16 [2048, 4096], P(('expert', 'rep')), may hold values from -6 to 6
- input_quant: bfloat16 [2048, 4096], P(('expert', 'rep')), may hold values from -6 to 6
- keep_mask: int32 [2048, 4096], P(('expert', 'rep')), may hold values 0 or 1
- grad_mixed: bfloat16 [2048, 4096], P(('expert', 'rep')), may hold values from -192 to 192
- gate_weight: bfloat16 [8, 4096, 7168], P('expert', None, 'rep'), may hold values from -0.09375 to 0.09375
- up_weight: bfloat16 [8, 4096, 7168], P('expert', None, 'rep'), may hold values from -0.09375 to 0.09375
- down_base: bfloat16 [8, 7168, 4096], P('expert', 'rep'), may hold values from -0.0625 to 0.0625
- down_round: bfloat16 [8, 7168, 4096], P('expert', 'rep'), may hold values from -8 to 8
- down_step: float32 [8, 4096], P('expert'), may hold values from 0.004 to 0.04
Outputs:
- mixed: bfloat16 [2048, 4096], P(('expert', 'rep'))
- round_grad: float32 [8, 7168, 4096], P('expert', 'rep')
Inputs may be any that keep to these rules, and one draw needn't show every extreme that they name: `route_ids`: within the 8 tokens of one device, each expert is named by at most 4 pairs; the two experts of a token differ.
All inputs are finite; a program needn't handle non-finite values. No bound on the sum of `keep_mask` on one device may be relied on, other than what follows from the above.
Results may differ from a plain program's by a relative error of at most 0.0065.
Values may be sent and summed in bfloat16 or wider, within the bound.
No kernel may reach another device: no remote copies, remote signals or barrier semaphores. Data moves between devices by JAX's collectives and lax.ppermute only.
A program may use at most 128 MiB of HBM per device.

v0:
```python
import jax
import jax.numpy as jnp
from jax import lax
from jax.sharding import PartitionSpec as P


def in_one_piece(arrays, axis, split_dim, concat_dim, along):
    both = jnp.concatenate(arrays, axis=along)
    filled, at, gathered = (
        lax.all_to_all(both, axis, split_axis=split_dim, concat_axis=concat_dim, tiled=True),
        0,
        [],
    )
    for a in arrays:
        gathered.append(lax.slice_in_dim(filled, at, at + a.shape[along], axis=along))
        at += a.shape[along]
    return tuple(gathered)


def sent_together(arrays, axis, dim, along):
    ends, at = ([], 0)
    for a in arrays[:-1]:
        at += a.shape[along]
        ends.append(at)
    both = jnp.concatenate(arrays, axis=along)
    return tuple(jnp.split(lax.all_gather(both, axis, axis=dim, tiled=True), ends, axis=along))


def local_slots(route_ids, experts):
    count = route_ids.shape[0]
    flat = route_ids.reshape(count * 2)
    onehot = (flat[:, None] == jnp.arange(experts, dtype=jnp.int32)[None, :]).astype(jnp.int32)
    before = jnp.cumsum(onehot, axis=0) - onehot
    return jnp.sum(before * onehot, axis=1).reshape(count, 2)


def body(
    route_ids,
    route_weight,
    input_float,
    input_quant,
    keep_mask,
    grad_mixed,
    gate_weight,
    up_weight,
    down_base,
    down_round,
    down_step,
):
    experts = lax.axis_size("expert")
    count = route_ids.shape[0]
    capacity = count // 2
    slot = local_slots(route_ids, experts)
    target = route_ids * capacity + slot
    columns = jnp.arange(experts * capacity, dtype=jnp.int32)
    first = (target[:, 0:1] == columns[None, :]).astype(jnp.float32)
    second = (target[:, 1:2] == columns[None, :]).astype(jnp.float32)
    placing = (first + second).astype(jnp.bfloat16)
    weighting = route_weight[:, 0:1] * first + route_weight[:, 1:2] * second
    x_in = jnp.where(keep_mask == 1, input_quant, input_float)
    send_rows = lax.dot_general(
        placing, x_in, (((0,), (0,)), ((), ())), preferred_element_type=jnp.float32
    ).astype(jnp.bfloat16)
    send_cot = lax.dot_general(
        weighting,
        grad_mixed.astype(jnp.float32),
        (((0,), (0,)), ((), ())),
        precision=lax.Precision.HIGHEST,
        preferred_element_type=jnp.float32,
    ).astype(jnp.bfloat16)
    own_rows, own_cot = in_one_piece((send_rows, send_cot), "expert", 0, 0, 1)
    w_gate = gate_weight[0]
    w_up = up_weight[0]
    soft = jax.nn.sigmoid(down_round[0].astype(jnp.float32))
    step_row = down_step[0][None, :]
    quant_down = (down_base[0].astype(jnp.float32) + step_row * soft).astype(jnp.bfloat16)
    all_rows, all_cot = sent_together((own_rows, own_cot), "rep", 0, 1)
    gate = jnp.dot(all_rows, w_gate, preferred_element_type=jnp.float32)
    up = jnp.dot(all_rows, w_up, preferred_element_type=jnp.float32)
    hidden = (jax.nn.silu(gate) * up).astype(jnp.bfloat16)
    grad_w = lax.dot_general(
        hidden, all_cot, (((0,), (0,)), ((), ())), preferred_element_type=jnp.float32
    )
    wide_down = lax.all_to_all(quant_down, "rep", split_axis=1, concat_axis=0, tiled=True)
    out_cols = jnp.dot(
        lax.all_gather(hidden, "rep", axis=1, tiled=True),
        wide_down,
        preferred_element_type=jnp.float32,
    )
    summed = lax.all_to_all(
        out_cols.astype(jnp.bfloat16), "rep", split_axis=0, concat_axis=1, tiled=True
    )
    returned = lax.all_to_all(summed, "expert", split_axis=0, concat_axis=0, tiled=True)
    mixed = jnp.dot(
        weighting,
        returned.astype(jnp.float32),
        precision=lax.Precision.HIGHEST,
        preferred_element_type=jnp.float32,
    ).astype(jnp.bfloat16)
    round_grad = (grad_w * step_row * soft * (1.0 - soft))[None]
    return (mixed, round_grad)


def solution(mesh):
    return jax.shard_map(
        body,
        mesh=mesh,
        in_specs=(
            P(("expert", "rep"), None),
            P(("expert", "rep"), None),
            P(("expert", "rep"), None),
            P(("expert", "rep"), None),
            P(("expert", "rep"), None),
            P(("expert", "rep"), None),
            P("expert", None, "rep"),
            P("expert", None, "rep"),
            P("expert", "rep", None),
            P("expert", "rep", None),
            P("expert", None),
        ),
        out_specs=(P(("expert", "rep"), None), P("expert", "rep", None)),
        check_vma=False,
    )
```

profile of v0, /device:TPU:1, one launch (start us, length us, event | category | flops | bytes accessed | tf_op | source)
XLA Modules:
  0.0 381.1 jit_solution(1803155560595772534)
XLA Ops:
  7.2 0.8 slice_bitcast_fusion.1
  8.1 0.8 copy.23
  9.5 1.3 convolution_convert_fusion.1
  10.8 1.3 convolution_convert_fusion
  12.3 14.9 %all_to_all.56 = bf16[8,4,8192]{2,1,0:T(4,128)(2,1)S(1)} all-to-all(bf16[8,4,8192]{2,1,0:T(4,128)(2,1)S(1)} %all_to_all.40), channel_id=1, replica_groups=mesh['expert'=8,'rep'=32] {'expert'}, dimensions={0} | all-to-all | bytes 1048576 | tf_op jit(solution)/shard_map/all_to_all | solution.py:10
  27.2 0.9 all_to_all.42
  28.2 139.6 %all-gather.3.cloned.1.call-done = bf16[1024,8192]{1,0:T(8,128)(2,1)} async-done(((bf16[32,8192]{1,0:T(8,128)(2,1)}), bf16[1024,8192]{1,0:T(8,128)(2,1)}) %all-gather.3.cloned.1.call-update) | async-done | bytes 16777232 | tf_op jit(solution)/shard_map/all_gather | solution.py:26
  167.8 6.1 %fusion.4 = f32[1024,224]{0,1:T(8,128)S(1)} fusion(bf16[1024,8192]{1,0:T(8,128)(2,1)} %all-gather.3.cloned.1.call-done, bf16[1,4096,224]{1,2,0:T(8,128)(2,1)S(1)} %copy-done), kind=kOutput, calls=%fused_computation.4 | convolution fusion | flops 1879048192 | bytes 11141120 | tf_op jit(solution)/shard_map/dot_general | solution.py:78
  174.0 2.0 copy-done.6
  176.5 3.5 fusion.28
  180.5 0.6 copy.27
  181.1 0.8 copy-done.3
  182.0 1.0 fusion.22
  182.9 0.6 copy.28
  183.6 0.9 fusion.19
  184.6 0.7 copy.25
  185.3 67.5 %all_to_all.57 = bf16[224,32,128]{2,0,1:T(8,128)(2,1)S(1)} all-to-all(bf16[224,32,128]{2,0,1:T(8,128)(2,1)S(1)} %copy.25), channel_id=1, replica_groups=mesh['expert'=8,'rep'=32] {'rep'}, dimensions={1} | all-to-all | bytes 3670016 | tf_op jit(solution)/shard_map/all_to_all | solution.py:84
  252.8 81.7 %all-gather.5.cloned.1.call-done = bf16[1024,7168]{0,1:T(8,128)(2,1)} async-done(((bf16[1024,224]{0,1:T(8,128)(2,1)}), bf16[1024,7168]{0,1:T(8,128)(2,1)}) %all-gather.5.cloned.1.call-update) | async-done | bytes 14680080 | tf_op jit(solution)/shard_map/all_gather | solution.py:86
  334.5 7.3 %convolution_convert_fusion.3 = bf16[1024,128]{1,0:T(8,128)(2,1)S(1)} fusion(bf16[1024,7168]{0,1:T(8,128)(2,1)} %all-gather.5.cloned.1.call-done, bf16[7168,128]{1,0:T(8,128)(2,1)S(1)} %bitcast.47), kind=kOutput, calls=%fused_computation.24 | convolution fusion | flops 1879179264 | bytes 16777216 | tf_op jit(solution)/shard_map/dot_general | solution.py:85
  341.9 17.4 %all_to_all.58 = bf16[32,32,128]{2,1,0:T(8,128)(2,1)S(1)} all-to-all(bf16[32,32,128]{2,1,0:T(8,128)(2,1)S(1)} %bitcast.49), channel_id=1, replica_groups=mesh['expert'=8,'rep'=32] {'rep'}, dimensions={0} | all-to-all | bytes 524288 | tf_op jit(solution)/shard_map/all_to_all | solution.py:90
  359.4 0.8 all_to_all.49
  360.2 4.8 %all-to-all-start.3 = ((bf16[8,4,4096]{2,1,0:T(4,128)(2,1)}), bf16[8,4,4096]{2,1,0:T(4,128)(2,1)S(1)}, u32[]{:S(2)}, u32[]{:S(2)}) async-start(bf16[8,4,4096]{2,1,0:T(4,128)(2,1)} %all_to_all.49), calls=%async_computation.3 | async-start | bytes 524288 | tf_op jit(solution)/shard_map/all_to_all | solution.py:93
  365.1 8.2 %fusion.15 = f32[1,224,4096]{2,1,0:T(8,128)} fusion(bf16[1024,224]{0,1:T(8,128)(2,1)S(1)} %copy-done.4, bf16[1024,8192]{1,0:T(8,128)(2,1)} %all-gather.3.cloned.1.call-done, f32[4096]{0:T(1024)S(1)} %bitcast.51, bf16[1,224,4096]{2,1,0:T(8,128)(2,1)} %param.20), kind=kOutput, calls=%fused_computation.9 | convolution fusion | flops 1886388224 | bytes 14368768 | tf_op jit(solution)/shard_map/dot_general | solution.py:81
  373.3 0.9 convolution_convert_fusion.2
  (31 shorter events, 2.2 us)
Async XLA Ops:
  7.2 160.7 %copy-start = (bf16[1,4096,224]{1,2,0:T(8,128)(2,1)S(1)}, bf16[1,4096,224]{1,2,0:T(8,128)(2,1)}, u32[]{:S(2)}) copy-start(bf16[1,4096,224]{1,2,0:T(8,128)(2,1)} %param.17) | copy-start | bytes 5505028
  7.2 160.6 %all-gather.3.cloned.1.call-start = ((), (), s32[]{:S(2)}) async-start(), calls=%async_computation.4 | async-start | bytes 17301504 | tf_op jit(solution)/shard_map/all_gather | solution.py:26
  28.2 306.3 %all-gather.5.cloned.1.call-start = ((), (), s32[]{:S(2)}) async-start(), calls=%async_computation.5 | async-start | bytes 15138816 | tf_op jit(solution)/shard_map/all_gather | solution.py:86
  167.8 8.2 %copy-start.6 = (bf16[1024,8192]{1,0:T(8,128)(2,1)S(1)}, bf16[1024,8192]{1,0:T(8,128)(2,1)}, u32[]{:S(2)}) copy-start(bf16[1024,8192]{1,0:T(8,128)(2,1)} %all-gather.3.cloned.1.call-done) | copy-start | bytes 50331652
  167.8 8.7 %copy-start.7 = (bf16[1,4096,224]{1,2,0:T(8,128)(2,1)S(1)}, bf16[1,4096,224]{1,2,0:T(8,128)(2,1)}, u32[]{:S(2)}) copy-start(bf16[1,4096,224]{1,2,0:T(8,128)(2,1)} %param.18) | copy-start | bytes 5505028
  176.5 3.6 copy-start.2
  180.5 1.5 copy-start.3
  182.9 0.7 copy-start.5
  334.5 30.5 %copy-start.4 = (bf16[1024,224]{0,1:T(8,128)(2,1)S(1)}, bf16[1024,224]{0,1:T(8,128)(2,1)}, u32[]{:S(2)}) copy-start(bf16[1024,224]{0,1:T(8,128)(2,1)} %fusion.28) | copy-start | bytes 1376260
  360.2 13.1 %all-to-all-start.3 = ((bf16[8,4,4096]{2,1,0:T(4,128)(2,1)}), bf16[8,4,4096]{2,1,0:T(4,128)(2,1)S(1)}, u32[]{:S(2)}, u32[]{:S(2)}) async-start(bf16[8,4,4096]{2,1,0:T(4,128)(2,1)} %all_to_all.49), calls=%async_computation.3 | async-start | bytes 524288 | tf_op jit(solution)/shard_map/all_to_all | solution.py:93
  365.0 9.2 %copy-start.1 = (bf16[1,4096,224]{1,2,0:T(8,128)(2,1)S(1)}, bf16[1,4096,224]{1,2,0:T(8,128)(2,1)}, u32[]{:S(2)}) copy-start(bf16[1,4096,224]{1,2,0:T(8,128)(2,1)} %param.17) | copy-start | bytes 5505028
Sparse Core Ops, SparseCore 0:
  28.3 139.4 all-gather.2
  180.2 154.3 all-gather.4
where the time goes:
time: 382 us; the launch traced here: 381 us
  waiting for transfers between devices  221 us (58%)
  blocking collectives  99.8 us (26%)
  matrix products  28.8 us (8%)
  between operations  14.2 us (4%)
  local copies, waits for them, and re-layouts  9.41 us (2%)
  starting transfers between devices  4.93 us (1%)
    all_gather x1, waiting for transfers between devices, sent_together(): lax.all_gather(both, axis, axis=dim, tiled=True)  140 us
    all_gather x1, waiting for transfers between devices, body(): lax.all_gather(hidden, 'rep', axis=1, tiled=True)  81.7 us
    all_to_all x1, blocking collectives, body(): lax.all_to_all(quant_down, 'rep', split_axis=1, concat_axis=0, tiled=True)  67.5 us
    all_to_all x1, blocking collectives, body(): lax.all_to_all(out_cols.astype(jnp.bfloat16), 'rep', split_axis=0, concat...  17.4 us
    all_to_all x1, blocking collectives, in_one_piece(): lax.all_to_all(both, axis, split_axis=split_dim, concat_axis=concat_dim,...  14.9 us
    dot_general x1, matrix products, body(): lax.dot_general(hidden, all_cot, (((0,), (0,)), ((), ())), preferred_elem...  8.21 us
  transfers between devices with their start and end apart: 3, of which 2 were waited for; matrix products, arithmetic and copies ran while one was open for 3% of the time, Pallas kernels for 0%

commit v1 on v0

--- a/solution.py
+++ b/solution.py
@@ -83,7 +83,7 @@
     )
     wide_down = lax.all_to_all(quant_down, "rep", split_axis=1, concat_axis=0, tiled=True)
     out_cols = jnp.dot(
-        lax.all_gather(hidden, "rep", axis=1, tiled=True),
+        jnp.concatenate(lax.all_gather(hidden, "rep"), axis=1),
         wide_down,
         preferred_element_type=jnp.float32,
     )

time: 382 us -> 399 us (1.045)
  blocking collectives: 99.8 us -> 32.3 us
  waiting for transfers between devices: 221 us -> 283 us
  local copies, waits for them, and re-layouts: 9.41 us -> 27.3 us
  starting transfers between devices: 4.93 us -> 9.63 us
    all_to_all x1 -> x0, blocking collectives: 67.5 us -> none  [body(): lax.all_to_all(quant_down, 'rep', split_axis=1, concat_axis=0, tiled=True)]
    all_gather x1, waiting for transfers between devices: 81.7 us -> 143 us  [body(): lax.all_gather(hidden, 'rep')]
    unnamed x19 -> x20, local copies, waits for them, and re-layouts: 5.48 us -> 22.1 us
    all_to_all x0 -> x1, starting transfers between devices: none -> 4.7 us  [body(): lax.all_to_all(quant_down, 'rep', split_axis=1, concat_axis=0, tiled=True)]
  transfers between devices with their start and end apart: 3 -> 4, of which waited for: 2 -> 2; matrix products, arithmetic and copies ran while one was open for 3% -> 8% of each run, Pallas kernels for 0% -> 0%
where the time goes in v1:
time: 399 us; the launch traced here: 398 us
  waiting for transfers between devices  283 us (71%)
  blocking collectives  32.3 us (8%)
  matrix products  28.9 us (7%)
  local copies, waits for them, and re-layouts  27.3 us (7%)
  between operations  14.2 us (4%)
  starting transfers between devices  9.63 us (2%)
    all_gather x1, waiting for transfers between devices, body(): lax.all_gather(hidden, 'rep')  143 us
    all_gather x1, waiting for transfers between devices, sent_together(): lax.all_gather(both, axis, axis=dim, tiled=True)  140 us
    unnamed x20, local copies, waits for them, and re-layouts  22.1 us
    all_to_all x1, blocking collectives, body(): lax.all_to_all(out_cols.astype(jnp.bfloat16), 'rep', split_axis=0, concat...  17.4 us
    all_to_all x1, blocking collectives, in_one_piece(): lax.all_to_all(both, axis, split_axis=split_dim, concat_axis=concat_dim,...  14.9 us
    dot_general x1, matrix products, body(): lax.dot_general(hidden, all_cot, (((0,), (0,)), ((), ())), preferred_elem...  8.21 us
  transfers between devices with their start and end apart: 4, of which 2 were waited for; matrix products, arithmetic and copies ran while one was open for 8% of the time, Pallas kernels for 0%

profile of v1, /device:TPU:1, one launch (start us, length us, event | category | flops | bytes accessed | tf_op | source)
XLA Modules:
  0.0 397.9 jit_solution(9273424431898968779)
XLA Ops:
  7.2 0.8 slice_bitcast_fusion.1
  8.1 0.8 copy.25
  9.5 1.3 convolution_convert_fusion.1
  10.8 1.3 convolution_convert_fusion
  12.3 14.9 %all_to_all.53 = bf16[8,4,8192]{2,1,0:T(4,128)(2,1)S(1)} all-to-all(bf16[8,4,8192]{2,1,0:T(4,128)(2,1)S(1)} %all_to_all.38), channel_id=1, replica_groups=mesh['expert'=8,'rep'=32] {'expert'}, dimensions={0} | all-to-all | bytes 1048576 | tf_op jit(solution)/shard_map/all_to_all | solution.py:10
  27.2 0.9 all_to_all.40
  28.2 139.6 %all-gather.4.cloned.1.call-done = bf16[1024,8192]{1,0:T(8,128)(2,1)} async-done(((bf16[32,8192]{1,0:T(8,128)(2,1)}), bf16[1024,8192]{1,0:T(8,128)(2,1)}) %all-gather.4.cloned.1.call-update) | async-done | bytes 16777232 | tf_op jit(solution)/shard_map/all_gather | solution.py:26
  167.8 6.1 %fusion.6 = f32[1024,224]{0,1:T(8,128)S(1)} fusion(bf16[1024,8192]{1,0:T(8,128)(2,1)} %all-gather.4.cloned.1.call-done, bf16[1,4096,224]{1,2,0:T(8,128)(2,1)S(1)} %copy-done), kind=kOutput, calls=%fused_computation.6 | convolution fusion | flops 1879048192 | bytes 11141120 | tf_op jit(solution)/shard_map/dot_general | solution.py:78
  174.0 2.0 copy-done.6
  176.5 3.5 fusion.32
  180.5 0.6 copy.31
  181.1 0.8 copy-done.3
  182.0 1.0 fusion.26
  183.7 0.9 fusion.21
  184.6 1.9 copy.27
  186.5 4.7 %all-to-all-start.1 = ((bf16[224,32,128]{2,0,1:T(8,128)(2,1)}), bf16[224,32,128]{2,0,1:T(8,128)(2,1)S(1)}, u32[]{:S(2)}, u32[]{:S(2)}) async-start(bf16[224,32,128]{2,0,1:T(8,128)(2,1)} %copy.27), calls=%async_computation.1 | async-start | bytes 3670016 | tf_op jit(solution)/shard_map/all_to_all | solution.py:84
  191.2 143.4 %all-gather.6.cloned.1.call-done = bf16[32768,224]{0,1:T(8,128)(2,1)} async-done(((bf16[1024,224]{0,1:T(8,128)(2,1)}), bf16[32768,224]{0,1:T(8,128)(2,1)}) %all-gather.6.cloned.1.call-update) | async-done | bytes 14680080 | tf_op jit(solution)/shard_map/all_gather | solution.py:86
  334.6 16.6 %copy.30 = bf16[28,8,32,1024]{3,2,1,0:T(8,128)(2,1)} copy(bf16[28,8,32,1024]{3,1,2,0:T(8,128)(2,1)} %bitcast.64) | data formatting | bytes 29360128
  351.2 7.4 %fusion.42 = bf16[1024,128]{1,0:T(8,128)(2,1)S(1)} fusion(bf16[224,32,128]{2,0,1:T(8,128)(2,1)S(1)} %all-to-all-done.1, bf16[32,1024,224]{1,0,2:T(8,128)(2,1)} %bitcast.65), kind=kOutput, calls=%fused_computation.29 | convolution fusion | flops 1879179264 | bytes 16777216 | tf_op jit(solution)/shard_map/dot_general | solution.py:85
  358.7 17.4 %all_to_all.54 = bf16[32,32,128]{2,1,0:T(8,128)(2,1)S(1)} all-to-all(bf16[32,32,128]{2,1,0:T(8,128)(2,1)S(1)} %bitcast.67), channel_id=1, replica_groups=mesh['expert'=8,'rep'=32] {'rep'}, dimensions={0} | all-to-all | bytes 524288 | tf_op jit(solution)/shard_map/all_to_all | solution.py:90
  376.2 0.8 all_to_all.46
  377.0 4.9 %all-to-all-start.3 = ((bf16[8,4,4096]{2,1,0:T(4,128)(2,1)}), bf16[8,4,4096]{2,1,0:T(4,128)(2,1)S(1)}, u32[]{:S(2)}, u32[]{:S(2)}) async-start(bf16[8,4,4096]{2,1,0:T(4,128)(2,1)} %all_to_all.46), calls=%async_computation.3 | async-start | bytes 524288 | tf_op jit(solution)/shard_map/all_to_all | solution.py:93
  381.8 8.2 %fusion.17 = f32[1,224,4096]{2,1,0:T(8,128)} fusion(bf16[1024,224]{0,1:T(8,128)(2,1)S(1)} %copy-done.4, bf16[1024,8192]{1,0:T(8,128)(2,1)} %all-gather.4.cloned.1.call-done, f32[4096]{0:T(1024)S(1)} %bitcast.69, bf16[1,224,4096]{2,1,0:T(8,128)(2,1)} %param.20), kind=kOutput, calls=%fused_computation.11 | convolution fusion | flops 1886388224 | bytes 14368768 | tf_op jit(solution)/shard_map/dot_general | solution.py:81
  390.1 0.9 convolution_convert_fusion.2
  (33 shorter events, 2.8 us)
Async XLA Ops:
  7.2 160.7 %copy-start = (bf16[1,4096,224]{1,2,0:T(8,128)(2,1)S(1)}, bf16[1,4096,224]{1,2,0:T(8,128)(2,1)}, u32[]{:S(2)}) copy-start(bf16[1,4096,224]{1,2,0:T(8,128)(2,1)} %param.17) | copy-start | bytes 5505028
  7.2 160.6 %all-gather.4.cloned.1.call-start = ((), (), s32[]{:S(2)}) async-start(), calls=%async_computation.4 | async-start | bytes 17301504 | tf_op jit(solution)/shard_map/all_gather | solution.py:26
  28.2 306.4 %all-gather.6.cloned.1.call-start = ((), (), s32[]{:S(2)}) async-start(), calls=%async_computation.5 | async-start | bytes 15138816 | tf_op jit(solution)/shard_map/all_gather | solution.py:86
  167.8 8.2 %copy-start.6 = (bf16[1024,8192]{1,0:T(8,128)(2,1)S(1)}, bf16[1024,8192]{1,0:T(8,128)(2,1)}, u32[]{:S(2)}) copy-start(bf16[1024,8192]{1,0:T(8,128)(2,1)} %all-gather.4.cloned.1.call-done) | copy-start | bytes 50331652
  167.8 8.7 %copy-start.7 = (bf16[1,4096,224]{1,2,0:T(8,128)(2,1)S(1)}, bf16[1,4096,224]{1,2,0:T(8,128)(2,1)}, u32[]{:S(2)}) copy-start(bf16[1,4096,224]{1,2,0:T(8,128)(2,1)} %param.18) | copy-start | bytes 5505028
  176.5 3.6 copy-start.2
  180.5 1.5 copy-start.3
  182.9 0.7 copy-start.5
  186.5 164.7 %all-to-all-start.1 = ((bf16[224,32,128]{2,0,1:T(8,128)(2,1)}), bf16[224,32,128]{2,0,1:T(8,128)(2,1)S(1)}, u32[]{:S(2)}, u32[]{:S(2)}) async-start(bf16[224,32,128]{2,0,1:T(8,128)(2,1)} %copy.27), calls=%async_computation.1 | async-start | bytes 3670016 | tf_op jit(solution)/shard_map/all_to_all | solution.py:84
  351.2 30.6 %copy-start.4 = (bf16[1024,224]{0,1:T(8,128)(2,1)S(1)}, bf16[1024,224]{0,1:T(8,128)(2,1)}, u32[]{:S(2)}) copy-start(bf16[1024,224]{0,1:T(8,128)(2,1)} %fusion.32) | copy-start | bytes 1376260
  377.0 13.1 %all-to-all-start.3 = ((bf16[8,4,4096]{2,1,0:T(4,128)(2,1)}), bf16[8,4,4096]{2,1,0:T(4,128)(2,1)S(1)}, u32[]{:S(2)}, u32[]{:S(2)}) async-start(bf16[8,4,4096]{2,1,0:T(4,128)(2,1)} %all_to_all.46), calls=%async_computation.3 | async-start | bytes 524288 | tf_op jit(solution)/shard_map/all_to_all | solution.py:93
  381.8 9.2 %copy-start.1 = (bf16[1,4096,224]{1,2,0:T(8,128)(2,1)S(1)}, bf16[1,4096,224]{1,2,0:T(8,128)(2,1)}, u32[]{:S(2)}) copy-start(bf16[1,4096,224]{1,2,0:T(8,128)(2,1)} %param.17) | copy-start | bytes 5505028
Sparse Core Ops, SparseCore 0:
  28.3 139.4 all-gather.3
  180.2 154.3 all-gather.5
